TPU v7x, 32 devices: a whole 2x2x4 slice. The times are simulated.
32 devices in a mesh: groups: 2 (over y), tensor: 4 (over z), frames: 4 (over x, core).
Axes of the slice: x: 2, y: 2, z: 4, core: 2. Of those that a mesh axis runs over, the one named last changes fastest.
Arguments:
- patches: bfloat16 [256, 16, 3072], P('tensor', ('groups', 'frames')), parts along dimension 1, may hold values from -12 to 12
- ln_gain: float32 [3072], replicated, may hold values from 0.5 to 1.5
- in_weight: bfloat16 [3072, 4, 768], P('frames', 'tensor'), may hold values from -0.109375 to 0.109375
- q_gain: float32 [4, 128], P('tensor'), may hold values from 0.1 to 1.9
- k_gain: float32 [4, 128], P('tensor'), may hold values from 0.1 to 1.9
- out_weight: bfloat16 [4, 512, 3072], P('tensor', None, 'frames'), may hold values from -0.25 to 0.25
Outputs:
- encoded: bfloat16 [256, 16, 3072], P('tensor', ('groups', 'frames')), parts along dimension 1
There are 2 independent parts, one for each index of `groups`. A program takes and returns all parts, laid end to end along the dimension named above; an argument that names none is the same for every part. Nothing has to cross between parts.
All inputs are finite; a program needn't handle non-finite values.
Results may differ from a plain program's by a relative error of at most 0.022.
Values may be sent and summed in bfloat16 or wider, within the bound.
No kernel may reach another device: no remote copies, remote signals or barrier semaphores. Data moves between devices by JAX's collectives and lax.ppermute only.
A program may use at most 64 MiB of HBM per device.

v0:
```python
import math
import jax
import jax.numpy as jnp
from jax import lax
from jax.sharding import PartitionSpec as P


def layer_norm(values, gain_vec):
    mean_val = jnp.mean(values, axis=-1, keepdims=True)
    centered = values - mean_val
    variance = jnp.mean(centered * centered, axis=-1, keepdims=True)
    return centered * lax.rsqrt(variance + 1e-06) * gain_vec


def local(patches, ln_gain, in_weight, q_gain, k_gain, out_weight):
    head_dim = q_gain.shape[1]
    normed = layer_norm(patches.astype(jnp.float32), ln_gain).astype(jnp.bfloat16)
    in_local = in_weight[:, 0, :]
    out_local = out_weight[0]
    every_patch = lax.all_gather(normed, "tensor", axis=0, tiled=True)
    joined_cols = jnp.einsum(
        "qye,ea->qya",
        every_patch,
        lax.all_gather(in_local, "frames", axis=0, tiled=True),
        preferred_element_type=jnp.float32,
    )
    query_slice = layer_norm(joined_cols[..., :head_dim], q_gain[0])
    key_slice = layer_norm(joined_cols[..., head_dim : 2 * head_dim], k_gain[0])
    value_slice = joined_cols[..., 2 * head_dim : 3 * head_dim]
    hidden = jax.nn.gelu(joined_cols[..., 3 * head_dim :], approximate=False)
    prepared = jnp.concatenate([query_slice, key_slice, value_slice, hidden], axis=-1).astype(
        jnp.bfloat16
    )
    query_slice = prepared[..., :head_dim]
    key_slice = prepared[..., head_dim : 2 * head_dim]
    value_slice = prepared[..., 2 * head_dim : 3 * head_dim]
    attention_logits = jnp.einsum(
        "ldg,bdg->dlb", query_slice, key_slice, preferred_element_type=jnp.float32
    ) * (1.0 / math.sqrt(head_dim))
    exponent_scores = jnp.exp(attention_logits)
    softmax_total = jnp.sum(exponent_scores, axis=-1)
    attention_output = jnp.einsum(
        "jdl,ljg->djg",
        exponent_scores.astype(jnp.bfloat16),
        value_slice,
        preferred_element_type=jnp.float32,
    )
    attention_output = attention_output / jnp.transpose(softmax_total)[:, :, None]
    blended_rows = jnp.concatenate(
        [attention_output.astype(jnp.bfloat16), prepared[..., 3 * head_dim :]], axis=-1
    )
    combined_output = lax.all_gather(out_local, "frames", axis=1, tiled=True)
    summed = lax.psum_scatter(
        jnp.einsum(
            "vto,ox->vtx", blended_rows, combined_output, preferred_element_type=jnp.float32
        ).astype(jnp.bfloat16),
        "tensor",
        scatter_dimension=0,
        tiled=True,
    ).astype(jnp.float32)
    return (patches.astype(jnp.float32) + summed).astype(jnp.bfloat16)


def solution(mesh):
    return jax.shard_map(
        local,
        mesh=mesh,
        in_specs=(
            P("tensor", ("groups", "frames"), None),
            P(),
            P("frames", "tensor", None),
            P("tensor", None),
            P("tensor", None),
            P("tensor", None, "frames"),
        ),
        out_specs=P("tensor", ("groups", "frames"), None),
        check_vma=False,
    )
```

profile of v0, /device:TPU:0, one launch (start us, length us, event | category | flops | bytes accessed | tf_op | source)
XLA Modules:
  0.0 220.3 jit_solution(9089769881547310153)
XLA Ops:
  6.5 0.0 copy-start
  6.5 0.0 copy-start.1
  6.5 0.0 all-gather.6.cloned.1.call-start
  6.5 1.4 convert_reduce_fusion
  7.9 1.5 fusion.5
  9.5 0.0 copy-done
  9.5 0.0 copy-done.1
  9.5 1.2 fusion.7
  10.7 0.0 all-gather.6.cloned.1.call-update
  10.7 0.0 all-gather.8.cloned.1.call-start
  10.8 0.7 all-gather.8.cloned.1.call-update
  11.5 0.0 all-gather.10.cloned.1.call-start
  11.5 0.7 all-gather.10.cloned.1.call-update
  12.2 0.0 copy-start.2
  12.2 0.0 copy-start.3
  12.2 0.0 reduce-scatter.2.cloned.1.call-start
  12.3 64.8 %all-gather.6.cloned.1.call-done = bf16[256,2,3072]{2,0,1:T(8,128)(2,1)} async-done(((bf16[64,2,3072]{2,0,1:T(8,128)(2,1)}), bf16[256,2,3072]{2,0,1:T(8,128)(2,1)}) %all-gather.6.cloned.1.call-update) | async-done | bytes 3145744 | tf_op jit(solution)/shard_map/all_gather | solution.py:20
  77.0 37.7 %all-gather.8.cloned.1.call-done = bf16[3072,1,768]{2,0,1:T(8,128)(2,1)} async-done(((bf16[768,1,768]{2,0,1:T(8,128)(2,1)}), bf16[3072,1,768]{2,0,1:T(8,128)(2,1)}) %all-gather.8.cloned.1.call-update) | async-done | bytes 4718608 | tf_op jit(solution)/shard_map/all_gather | solution.py:24
  114.7 5.9 %fusion = f32[256,2,768]{2,0,1:T(8,128)S(1)} fusion(bf16[256,2,3072]{2,0,1:T(8,128)(2,1)} %all-gather.6.cloned.1.call-done, bf16[3072,1,768]{2,0,1:T(8,128)(2,1)} %all-gather.8.cloned.1.call-done), kind=kOutput, calls=%fused_computation | convolution fusion | flops 2415919104 | bytes 9437184 | tf_op jit(solution)/shard_map/qye,ea->qya/dot_general | solution.py:21
  120.6 0.2 slice_reduce_fusion.1
  120.8 0.4 multiply_reduce_fusion.1
  121.2 0.0 copy-done.2
  121.3 0.0 copy-done.3
  121.3 0.5 fusion.33
  121.8 0.3 fusion.11
  122.0 1.7 fusion.14
  123.8 21.1 %all-gather.10.cloned.1.call-done = bf16[1,512,3072]{2,1,0:T(8,128)(2,1)} async-done(((bf16[1,512,768]{2,1,0:T(8,128)(2,1)}), bf16[1,512,3072]{2,1,0:T(8,128)(2,1)}) %all-gather.10.cloned.1.call-update) | async-done | bytes 3145744 | tf_op jit(solution)/shard_map/all_gather | solution.py:52
  144.8 5.4 %convolution_convert_fusion = bf16[256,2,3072]{2,0,1:T(8,128)(2,1)} fusion(bf16[1,512,3072]{2,1,0:T(8,128)(2,1)} %all-gather.10.cloned.1.call-done, bf16[256,2,384]{2,0,1:T(8,128)(2,1)S(1)} %fusion.14, bf16[256,2,128]{2,0,1:T(8,128)(2,1)S(1)} %fusion.11), kind=kOutput, calls=%fused_computation.2 | convolution fusion | flops 1613234176 | bytes 6815744 | tf_op jit(solution)/shard_map/vto,ox->vtx/dot_general | solution.py:54
  150.2 0.0 reduce-scatter.2.cloned.1.call-update
  150.2 60.6 %reduce-scatter.2.cloned.1.call-done = bf16[64,2,3072]{2,0,1:T(8,128)(2,1)} async-done(((bf16[256,2,3072]{2,0,1:T(8,128)(2,1)}), bf16[64,2,3072]{2,0,1:T(8,128)(2,1)}) %reduce-scatter.2.cloned.1.call-update) | async-done | bytes 786448 | tf_op jit(solution)/shard_map/reduce_scatter | solution.py:53
  210.8 1.3 fusion.8
  212.1 1.7 copy.8
  (5 shorter events, 0.0 us)
Async XLA Ops:
  6.5 2.9 %copy-start = (bf16[64,2,3072]{2,1,0:T(2,128)(2,1)S(1)}, bf16[64,2,3072]{2,1,0:T(2,128)(2,1)}, u32[]{:S(2)}) copy-start(bf16[64,2,3072]{2,1,0:T(2,128)(2,1)} %param.6) | copy-start | bytes 2359300
  6.5 2.9 %copy-start.1 = (f32[3072]{0:T(1024)S(1)}, f32[3072]{0:T(1024)}, u32[]{:S(2)}) copy-start(f32[3072]{0:T(1024)} %param.7) | copy-start | bytes 36868
  6.5 70.5 %all-gather.6.cloned.1.call-start = ((), (), s32[]{:S(2)}) async-start(), calls=%async_computation.1 | async-start | bytes 3932160 | tf_op jit(solution)/shard_map/all_gather | solution.py:20
  10.7 104.0 %all-gather.8.cloned.1.call-start = ((), (), s32[]{:S(2)}) async-start(), calls=%async_computation.3 | async-start | bytes 5898240 | tf_op jit(solution)/shard_map/all_gather | solution.py:24
  11.5 133.3 %all-gather.10.cloned.1.call-start = ((), (), s32[]{:S(2)}) async-start(), calls=%async_computation.4 | async-start | bytes 3932160 | tf_op jit(solution)/shard_map/all_gather | solution.py:52
  12.2 109.0 %copy-start.2 = (f32[1,128]{1,0:T(1,128)S(1)}, f32[1,128]{1,0:T(1,128)}, u32[]{:S(2)}) copy-start(f32[1,128]{1,0:T(1,128)} %param.10) | copy-start | bytes 1540
  12.2 109.0 %copy-start.3 = (f32[1,128]{1,0:T(1,128)S(1)}, f32[1,128]{1,0:T(1,128)}, u32[]{:S(2)}) copy-start(f32[1,128]{1,0:T(1,128)} %param.9) | copy-start | bytes 1540
  12.2 198.5 %reduce-scatter.2.cloned.1.call-start = ((), (), s32[]{:S(2)}) async-start(), calls=%async_computation.2 | async-start | bytes 3932160 | tf_op jit(solution)/shard_map/reduce_scatter | solution.py:53
Sparse Core Ops, SparseCore 0:
  10.8 66.1 all-gather.5
  78.6 36.0 all-gather.7
  116.3 28.5 all-gather.9
  150.3 60.3 reduce-scatter.1
where the time goes:
time: 221 us; the launch traced here: 220 us
  waiting for transfers between devices  185 us (84%)
  between operations  13.2 us (6%)
  matrix products  12 us (5%)
  other arithmetic  7.81 us (4%)
    all_gather x1, waiting for transfers between devices, local(): every_patch = lax.all_gather(normed, 'tensor', axis=0, tiled=True)  64.8 us
    reduce_scatter x1, waiting for transfers between devices, local(): lax.psum_scatter(jnp.einsum('vto,ox->vtx', blended_rows, combined_output,...  60.6 us
    all_gather x1, waiting for transfers between devices, local(): lax.all_gather(in_local, 'frames', axis=0, tiled=True)  37.7 us
    all_gather x1, waiting for transfers between devices, local(): combined_output = lax.all_gather(out_local, 'frames', axis=1, tiled=True)  21.1 us
    dot_general x1, matrix products, local(): jnp.einsum('qye,ea->qya', every_patch, lax.all_gather(in_local, 'frames',...  5.89 us
    dot_general x1, matrix products, local(): jnp.einsum('vto,ox->vtx', blended_rows, combined_output, preferred_elemen...  5.36 us
  transfers between devices with their start and end apart: 4, of which 4 were waited for; matrix products, arithmetic and copies ran while one was open for 4% of the time, Pallas kernels for 0%

commit v1 on v0

--- a/solution.py
+++ b/solution.py
@@ -3,6 +3,14 @@
 import jax.numpy as jnp
 from jax import lax
 from jax.sharding import PartitionSpec as P
+
+
+def lay_ports(page, row_dim):
+    page = jnp.moveaxis(page, 0, row_dim)
+    carry_out = page.shape
+    return page.reshape(
+        *carry_out[:row_dim], carry_out[row_dim] * carry_out[row_dim + 1], *carry_out[row_dim + 2 :]
+    )
 
 
 def layer_norm(values, gain_vec):
@@ -49,10 +57,38 @@
     blended_rows = jnp.concatenate(
         [attention_output.astype(jnp.bfloat16), prepared[..., 3 * head_dim :]], axis=-1
     )
-    combined_output = lax.all_gather(out_local, "frames", axis=1, tiled=True)
+
+    def wait_copies(original, axis_id, where_dim, x_in, pos_dim):
+        z_new, tmp, t1 = (
+            jax.lax.axis_size(axis_id),
+            jax.lax.axis_index(axis_id),
+            original.shape[where_dim],
+        )
+        sides = tuple(((at, (at + 1) % z_new) for at in range(z_new)))
+        slots = tuple(((at, (at - 1) % z_new) for at in range(z_new)))
+        r_now = {}
+        local_next = z_new // 2
+        high = back = original
+        for dev in range(local_next + 1):
+            before = jax.lax.ppermute(high, axis_id, sides) if dev < local_next else None
+            fresh = jax.lax.ppermute(back, axis_id, slots) if dev < z_new - local_next - 1 else None
+            r_now[-dev] = x_in(high, (tmp - dev) % z_new * t1)
+            if 0 < dev < z_new - local_next:
+                r_now[dev] = x_in(back, (tmp + dev) % z_new * t1)
+            high, back = (before, fresh)
+        r_now = jnp.stack(tuple((r_now[idx] for idx in sorted(r_now))), axis=0)
+        r_now = r_now[(jnp.arange(z_new) - tmp + local_next) % z_new]
+        return lay_ports(r_now, pos_dim)
+
     summed = lax.psum_scatter(
-        jnp.einsum(
-            "vto,ox->vtx", blended_rows, combined_output, preferred_element_type=jnp.float32
+        wait_copies(
+            out_local,
+            "frames",
+            1,
+            lambda own_block, offset: jnp.einsum(
+                "vto,ox->vtx", blended_rows, own_block, preferred_element_type=jnp.float32
+            ),
+            pos_dim=2,
         ).astype(jnp.bfloat16),
         "tensor",
         scatter_dimension=0,

time: 221 us -> 203 us (0.919)
  waiting for transfers between devices: 185 us -> 159 us
  local copies, waits for them, and re-layouts: 1.71 us -> 8.15 us
  starting transfers between devices: 0.12 us -> 5.06 us
  matrix products: 12 us -> 8.99 us
    all_gather x1 -> x0, waiting for transfers between devices: 21.1 us -> none  [local(): combined_output = lax.all_gather(out_local, 'frames', axis=1, tiled=True)]
    all_gather x1, waiting for transfers between devices: 64.8 us -> 45.1 us  [local(): every_patch = lax.all_gather(normed, 'tensor', axis=0, tiled=True)]
    ppermute x0 -> x3, waiting for transfers between devices: none -> 15.4 us  [the longest x2 15.4 us: wait_copies(): jax.lax.ppermute(high, axis_id, sides)]
    ppermute x0 -> x3, starting transfers between devices: none -> 4.98 us  [the longest x2 3 us: wait_copies(): jax.lax.ppermute(high, axis_id, sides)]
    convert_element_type x0 -> x1, local copies, waits for them, and re-layouts: none -> 3.98 us  [local(): summed = lax.psum_scatter(wait_copies(out_local, 'frames', 1, lambda own_...]
    dot_general x1 -> x4, matrix products: 5.36 us -> 2.33 us  [local(): jnp.einsum('vto,ox->vtx', blended_rows, own_block, preferred_element_type...]
    gather x0 -> x1, local copies, waits for them, and re-layouts: none -> 2.45 us  [wait_copies(): r_now = r_now[(jnp.arange(z_new) - tmp + local_next) % z_new]]
  transfers between devices with their start and end apart: 4 -> 6, of which waited for: 4 -> 4; matrix products, arithmetic and copies ran while one was open for 4% -> 5% of each run, Pallas kernels for 0% -> 0%
where the time goes in v1:
time: 203 us
  waiting for transfers between devices  159 us (78%)
  between operations  13.3 us (7%)
  matrix products  8.99 us (4%)
  other arithmetic  8.27 us (4%)
  local copies, waits for them, and re-layouts  8.15 us (4%)
  starting transfers between devices  5.06 us (2%)
    reduce_scatter x1, waiting for transfers between devices, local(): lax.psum_scatter(wait_copies(out_local, 'frames', 1, lambda own_block, of...  60.6 us
    all_gather x1, waiting for transfers between devices, local(): every_patch = lax.all_gather(normed, 'tensor', axis=0, tiled=True)  45.1 us
    all_gather x1, waiting for transfers between devices, local(): lax.all_gather(in_local, 'frames', axis=0, tiled=True)  37.7 us
    ppermute x2, waiting for transfers between devices, wait_copies(): jax.lax.ppermute(high, axis_id, sides)  15.4 us
    dot_general x1, matrix products, local(): jnp.einsum('qye,ea->qya', every_patch, lax.all_gather(in_local, 'frames',...  5.89 us
  transfers between devices with their start and end apart: 6, of which 4 were waited for; matrix products, arithmetic and copies ran while one was open for 5% of the time, Pallas kernels for 0%

profile of v1, /device:TPU:0, one launch (start us, length us, event | category | flops | bytes accessed | tf_op | source)
XLA Modules:
  0.0 203.2 jit_solution(2506508884416657072)
XLA Ops:
  6.5 0.0 copy-start
  6.5 0.0 copy-start.2
  6.5 0.0 all-gather.4.cloned.1.call-start
  6.5 1.4 convert_reduce_fusion
  7.9 1.5 fusion.4
  9.5 0.0 copy-done
  9.5 0.0 copy-done.2
  9.5 0.0 copy-start.3
  9.5 1.2 fusion.6
  10.7 0.0 all-gather.4.cloned.1.call-update
  10.7 0.0 all-gather.6.cloned.1.call-start
  10.8 0.7 all-gather.6.cloned.1.call-update
  11.5 0.0 reduce-scatter.2.cloned.1.call-start
  11.5 0.0 copy-done.3
  11.5 0.5 collective-permute-start
  12.1 2.0 collective-permute-start.2
  14.1 15.4 %collective-permute-done = bf16[512,768]{1,0:T(8,128)(2,1)S(1)} collective-permute-done((bf16[512,768]{1,0:T(8,128)(2,1)S(1)}, bf16[512,768]{1,0:T(8,128)(2,1)S(1)}, u32[]{:S(2)}, u32[]{:S(2)}) %collective-permute-start) | collective-permute-done | bytes 786464 | tf_op jit(solution)/shard_map/ppermute | solution.py:73
  29.5 2.5 %collective-permute-start.1 = (bf16[512,768]{1,0:T(8,128)(2,1)S(1)}, bf16[512,768]{1,0:T(8,128)(2,1)S(1)}, u32[]{:S(2)}, u32[]{:S(2)}) collective-permute-start(bf16[512,768]{1,0:T(8,128)(2,1)S(1)} %collective-permute-done), channel_id=1, source_target_pairs={{0,1},{1,2},{2,3},{3,0},{4,5},{5,6},{6,7},{7,4},{8,9},{9,10},{10,1... | collective-permute-start | bytes 2359304 | tf_op jit(solution)/shard_map/ppermute | solution.py:73
  32.0 45.1 %all-gather.4.cloned.1.call-done = bf16[256,2,3072]{2,0,1:T(8,128)(2,1)} async-done(((bf16[64,2,3072]{2,0,1:T(8,128)(2,1)}), bf16[256,2,3072]{2,0,1:T(8,128)(2,1)}) %all-gather.4.cloned.1.call-update) | async-done | bytes 3145744 | tf_op jit(solution)/shard_map/all_gather | solution.py:28
  77.1 37.7 %all-gather.6.cloned.1.call-done = bf16[3072,1,768]{2,0,1:T(8,128)(2,1)} async-done(((bf16[768,1,768]{2,0,1:T(8,128)(2,1)}), bf16[3072,1,768]{2,0,1:T(8,128)(2,1)}) %all-gather.6.cloned.1.call-update) | async-done | bytes 4718608 | tf_op jit(solution)/shard_map/all_gather | solution.py:32
  114.7 5.9 %fusion = f32[256,2,768]{2,0,1:T(8,128)S(1)} fusion(bf16[256,2,3072]{2,0,1:T(8,128)(2,1)} %all-gather.4.cloned.1.call-done, bf16[3072,1,768]{2,0,1:T(8,128)(2,1)} %all-gather.6.cloned.1.call-done), kind=kOutput, calls=%fused_computation.2 | convolution fusion | flops 2415919104 | bytes 9437184 | tf_op jit(solution)/shard_map/qye,ea->qya/dot_general | solution.py:29
  120.6 0.0 copy-start.4
  120.6 0.0 copy-start.5
  120.6 0.2 slice_reduce_fusion.1
  120.9 1.7 fusion.13
  122.6 0.4 multiply_reduce_fusion.1
  123.0 0.0 copy-done.4
  123.0 0.0 copy-done.5
  123.0 0.5 fusion.34
  123.5 0.3 fusion.10
  123.8 0.6 convolution_bitcast_fusion.1
  124.4 0.6 convolution_bitcast_fusion.2
  125.0 0.0 collective-permute-done.1
  125.0 0.6 convolution_bitcast_fusion.3
  125.6 0.0 collective-permute-done.2
  125.6 0.6 convolution_bitcast_fusion
  126.2 0.4 pad_maximum_fusion
  126.6 2.5 %gather_fusion = bf16[4,256,2,768]{3,1,2,0:T(8,128)(2,1)} fusion(bf16[4,256,2,768]{3,1,2,0:T(8,128)(2,1)S(1)} %pad_maximum_fusion, s32[1024]{0:T(1024)S(1)} %pad_clamp_fusion), kind=kCustom, calls=%fused_computation | custom fusion | bytes 6291472 | tf_op jit(solution)/shard_map/gather | solution.py:80
  129.1 4.0 %copy.16 = bf16[4,2,32,8,768]{4,3,0,2,1:T(8,128)(2,1)} copy(bf16[4,2,32,8,768]{4,3,2,1,0:T(8,128)(2,1)} %bitcast.44) | data formatting | bytes 6291456 | tf_op jit(solution)/shard_map/convert_element_type | solution.py:92
  133.1 0.0 copy-start.1
  133.1 0.0 reduce-scatter.2.cloned.1.call-update
  133.1 60.6 %reduce-scatter.2.cloned.1.call-done = bf16[64,2,3072]{2,0,1:T(8,128)(2,1)} async-done(((bf16[256,2,3072]{2,0,1:T(8,128)(2,1)}), bf16[64,2,3072]{2,0,1:T(8,128)(2,1)}) %reduce-scatter.2.cloned.1.call-update) | async-done | bytes 786448 | tf_op jit(solution)/shard_map/reduce_scatter | solution.py:83
  193.6 0.0 copy-done.1
  193.6 1.3 fusion.7
  195.0 1.7 copy.12
  (7 shorter events, 0.1 us)
Async XLA Ops:
  6.5 2.9 %copy-start = (bf16[64,2,3072]{2,1,0:T(2,128)(2,1)S(1)}, bf16[64,2,3072]{2,1,0:T(2,128)(2,1)}, u32[]{:S(2)}) copy-start(bf16[64,2,3072]{2,1,0:T(2,128)(2,1)} %param.6) | copy-start | bytes 2359300
  6.5 2.9 %copy-start.2 = (f32[3072]{0:T(1024)S(1)}, f32[3072]{0:T(1024)}, u32[]{:S(2)}) copy-start(f32[3072]{0:T(1024)} %param.7) | copy-start | bytes 36868
  6.5 70.5 %all-gather.4.cloned.1.call-start = ((), (), s32[]{:S(2)}) async-start(), calls=%async_computation.1 | async-start | bytes 3932160 | tf_op jit(solution)/shard_map/all_gather | solution.py:28
  9.5 2.1 %copy-start.3 = (bf16[1,512,768]{2,1,0:T(8,128)(2,1)S(1)}, bf16[1,512,768]{2,1,0:T(8,128)(2,1)}, u32[]{:S(2)}) copy-start(bf16[1,512,768]{2,1,0:T(8,128)(2,1)} %param.11) | copy-start | bytes 2359300
  10.7 104.0 %all-gather.6.cloned.1.call-start = ((), (), s32[]{:S(2)}) async-start(), calls=%async_computation.3 | async-start | bytes 5898240 | tf_op jit(solution)/shard_map/all_gather | solution.py:32
  11.5 182.1 %reduce-scatter.2.cloned.1.call-start = ((), (), s32[]{:S(2)}) async-start(), calls=%async_computation.2 | async-start | bytes 3932160 | tf_op jit(solution)/shard_map/reduce_scatter | solution.py:83
  11.5 18.0 %collective-permute-start = (bf16[512,768]{1,0:T(8,128)(2,1)S(1)}, bf16[512,768]{1,0:T(8,128)(2,1)S(1)}, u32[]{:S(2)}, u32[]{:S(2)}) collective-permute-start(bf16[512,768]{1,0:T(8,128)(2,1)S(1)} %bitcast.45), channel_id=1, source_target_pairs={{0,1},{1,2},{2,3},{3,0},{4,5},{5,6},{6,7},{7,4},{8,9},{9,10},{10,1... | collective-permute-start | bytes 2359304 | tf_op jit(solution)/shard_map/ppermute | solution.py:73
  12.1 113.5 %collective-permute-start.2 = (bf16[512,768]{1,0:T(8,128)(2,1)S(1)}, bf16[512,768]{1,0:T(8,128)(2,1)S(1)}, u32[]{:S(2)}, u32[]{:S(2)}) collective-permute-start(bf16[512,768]{1,0:T(8,128)(2,1)S(1)} %bitcast.46), channel_id=1, source_target_pairs={{0,3},{1,0},{2,1},{3,2},{4,7},{5,4},{6,5},{7,6},{8,11},{9,8},{10,9... | collective-permute-start | bytes 2359304 | tf_op jit(solution)/shard_map/ppermute | solution.py:74
  29.5 95.5 %collective-permute-start.1 = (bf16[512,768]{1,0:T(8,128)(2,1)S(1)}, bf16[512,768]{1,0:T(8,128)(2,1)S(1)}, u32[]{:S(2)}, u32[]{:S(2)}) collective-permute-start(bf16[512,768]{1,0:T(8,128)(2,1)S(1)} %collective-permute-done), channel_id=1, source_target_pairs={{0,1},{1,2},{2,3},{3,0},{4,5},{5,6},{6,7},{7,4},{8,9},{9,10},{10,1... | collective-permute-start | bytes 2359304 | tf_op jit(solution)/shard_map/ppermute | solution.py:73
  120.6 2.4 %copy-start.4 = (f32[1,128]{1,0:T(1,128)S(1)}, f32[1,128]{1,0:T(1,128)}, u32[]{:S(2)}) copy-start(f32[1,128]{1,0:T(1,128)} %param.10) | copy-start | bytes 1540
  120.6 2.4 %copy-start.5 = (f32[1,128]{1,0:T(1,128)S(1)}, f32[1,128]{1,0:T(1,128)}, u32[]{:S(2)}) copy-start(f32[1,128]{1,0:T(1,128)} %param.9) | copy-start | bytes 1540
  133.1 60.6 %copy-start.1 = (bf16[64,2,3072]{2,1,0:T(2,128)(2,1)S(1)}, bf16[64,2,3072]{2,1,0:T(2,128)(2,1)}, u32[]{:S(2)}) copy-start(bf16[64,2,3072]{2,1,0:T(2,128)(2,1)} %param.6) | copy-start | bytes 2359300
Sparse Core Ops, SparseCore 0:
  10.9 66.1 all-gather.3
  78.6 36.0 all-gather.5
  133.2 60.3 reduce-scatter.1
